TPU v7x, 32 devices: a whole 2x2x4 slice. The times are simulated.
32 devices in a mesh: seq: 8 (over y, x, core), tensor: 4 (over z).
Axes of the slice: x: 2, y: 2, z: 4, core: 2. Of those that a mesh axis runs over, the one named last changes fastest.
Arguments:
- queries: bfloat16 [1024, 4096], P(('seq', 'tensor')), may hold values from -5 to 5
- keys: bfloat16 [1024, 1024], P(('seq', 'tensor')), may hold values from -5 to 5
- values: bfloat16 [1024, 1024], P(('seq', 'tensor')), may hold values from -5 to 5
- mamba_x: bfloat16 [1024, 8192], P(('seq', 'tensor')), may hold values from -5 to 5
- mamba_b: bfloat16 [1024, 1024], P(('seq', 'tensor')), may hold values from -5 to 5
- mamba_c: bfloat16 [1024, 1024], P(('seq', 'tensor')), may hold values from -5 to 5
- mamba_dt: bfloat16 [1024, 128], P(('seq', 'tensor')), may hold values from -4 to 4
- conv_x: bfloat16 [4, 8192], P(None, 'tensor'), may hold values from -3 to 3
- conv_b: bfloat16 [4, 1024], P(None, 'tensor'), may hold values from -3 to 3
- conv_c: bfloat16 [4, 1024], P(None, 'tensor'), may hold values from -3 to 3
- dt_bias: float32 [128], P('tensor'), may hold values from -1 to 1
- decay_rate: float32 [128], P('tensor'), may hold values from 0.0001 to 0.05
- skip_gain: float32 [128], P('tensor'), may hold values from 0.5 to 1.5
- norm_gain: float32 [8192], P('tensor'), may hold values from 0.5 to 1.5
- windows: int32 [32], replicated, may hold values from 160 to 640, as said below
- doc_lengths: int32 [3], replicated, may hold values from 1 to 768, 1024 in all
Outputs:
- attn_out: bfloat16 [1024, 4096], P('seq', 'tensor')
- mamba_out: bfloat16 [1024, 8192], P('seq', 'tensor')
- attn_checksum: float32 [4096], P('tensor')
- mamba_checksum: float32 [8192], P('tensor')
Inputs may be any that keep to these rules, and one draw needn't show every extreme that they name: `windows`: one of the 32 query heads has a window of exactly 640 tokens. `doc_lengths`: 3 lengths summing to 1024; the longest is exactly three quarters of 1024.
All inputs are finite; a program needn't handle non-finite values.
Results may differ from a plain program's by a relative error of at most 0.007.
Values may be sent and summed in bfloat16 or wider, within the bound.
A program may use at most 192 MiB of HBM per device.

v0:
```python
import math

import jax
import jax.numpy as jnp
from jax import lax
from jax.sharding import PartitionSpec as P

HEAD_SIZE = 128
MP = 64
MN = 128
KC = 4


NEG_LARGE = -1e30
EPS_NORM = 1e-05


def shifted(block, axis, distance):
    devices = range(lax.axis_size(axis))
    route = [(i - distance, i) for i in devices if i - distance in devices]
    return lax.ppermute(block, axis, route)


def prefix(x, axis, combine, identity):
    length, here = (lax.axis_size(axis), lax.axis_index(axis))
    everything = jax.tree.map(
        lambda part, kind: lax.all_gather(part.astype(kind), axis), x, (jnp.bfloat16, jnp.bfloat16)
    )
    start = jax.tree.map(
        lambda part, zero: jnp.broadcast_to(jnp.asarray(zero, part.dtype), part.shape), x, identity
    )

    def turn(k, before):
        reached = k < here
        new = combine(
            before, jax.tree.map(lambda part, own: part[k].astype(own.dtype), everything, x)
        )
        return jax.tree.map(lambda a, b: jnp.where(reached, a, b), new, before)

    return lax.fori_loop(0, length, turn, start)


def doc_table(doc_lengths):
    return jnp.cumsum(doc_lengths) - doc_lengths


def doc_index(positions, doc_starts):
    return jnp.sum((positions[:, None] >= doc_starts[None, :]).astype(jnp.int32), axis=1) - 1


def allowed_mask(query_pos, key_pos, doc_starts, window_per_head):
    gap = query_pos[:, None] - key_pos[None, :]
    same_doc = doc_index(query_pos, doc_starts)[:, None] == doc_index(key_pos, doc_starts)[None, :]
    base_ok = (gap >= 0) & (key_pos[None, :] >= 0) & same_doc
    return base_ok[None, None] & (gap[None, None] < window_per_head[:, :, None, None])


def attend_piece(
    carry, piece, key_start, grouped_heads, query_pos, doc_starts, window_per_head, reach
):
    key_rows, value_rows = piece
    key_count = key_rows.shape[0]
    shared_heads = grouped_heads.shape[1]
    key_pos = jnp.arange(key_count, dtype=jnp.int32)

    def compute(state):
        old_max, old_total, old_accum = state
        keys_rank3 = key_rows.reshape(key_count, shared_heads, HEAD_SIZE)
        values_rank3 = value_rows.reshape(key_count, shared_heads, HEAD_SIZE)
        scores = jnp.einsum(
            "tgqd,sgd->gqts", grouped_heads, keys_rank3, preferred_element_type=jnp.float32
        ) * (1.0 / math.sqrt(HEAD_SIZE))
        allowed = allowed_mask(query_pos, key_pos, doc_starts, window_per_head)
        scores = jnp.where(allowed, scores, NEG_LARGE)
        new_max = jnp.maximum(old_max, jnp.max(scores, axis=-1))
        weights = jnp.where(allowed, jnp.exp(scores - new_max[..., None]), 0.0)
        new_total = jnp.sum(weights, axis=-1)
        product = jnp.einsum(
            "gqts,sgd->gqtd",
            weights.astype(jnp.bfloat16),
            values_rank3,
            preferred_element_type=jnp.float32,
        )
        return (new_max, new_total, product)

    touches = (key_start + key_count - 1 >= query_pos[0] - reach) & (key_start <= query_pos[-1])
    return lax.cond(touches, compute, lambda state: state, carry)


def causal_conv(extended, taps, positions, doc_starts):
    count = positions.shape[0]
    docs_out = doc_index(positions, doc_starts)
    ext_pos = positions[0] - (KC - 1) + jnp.arange(count + KC - 1, dtype=jnp.int32)
    docs_ext = doc_index(ext_pos, doc_starts)
    running = jnp.zeros((count, extended.shape[1]), jnp.float32)
    for tap_index in range(KC):
        offset = KC - 1 - tap_index
        valid = (docs_ext[offset : offset + count] == docs_out) & (
            ext_pos[offset : offset + count] >= 0
        )
        term = taps[tap_index].astype(jnp.float32)[None, :] * extended[
            offset : offset + count
        ].astype(jnp.float32)
        running = running + jnp.where(valid[:, None], term, 0.0)
    return jax.nn.silu(running).astype(jnp.bfloat16)


def stretch_terms(x_rows, b_rows, c_rows, dt_rows, positions, doc_starts, dt_bias, decay_rate):
    count = positions.shape[0]
    heads = x_rows.shape[1] // MP
    groups = b_rows.shape[1] // MN
    per_group = heads // groups
    docs = doc_index(positions, doc_starts)
    prior_doc = doc_index(positions[:1] - 1, doc_starts)[0]
    delta = jax.nn.softplus(dt_rows.astype(jnp.float32) + dt_bias[None, :])
    log_decay = -delta * decay_rate[None, :]
    running = jnp.cumsum(log_decay, axis=0)
    running_heads = running.T
    order = jnp.arange(count, dtype=jnp.int32)
    causal = order[:, None] >= order[None, :]
    same_doc = docs[:, None] == docs[None, :]
    gaps = running_heads[:, :, None] - running_heads[:, None, :]
    segment = jnp.where((causal & same_doc)[None], jnp.exp(jnp.minimum(gaps, 0.0)), 0.0)
    inputs3 = x_rows.reshape(count, heads, MP)
    b_groups = b_rows.reshape(count, groups, MN)
    c_groups = c_rows.reshape(count, groups, MN)
    cross = jnp.einsum("tgn,sgn->gts", c_groups, b_groups, preferred_element_type=jnp.float32)
    cross_heads = jnp.repeat(cross, per_group, axis=0)
    mixing = (segment * cross_heads * delta.T[:, None, :]).astype(jnp.bfloat16)
    intra = jnp.einsum("hts,shp->thp", mixing, inputs3, preferred_element_type=jnp.float32)
    last_doc = docs[count - 1]
    to_end = (
        jnp.where((docs == last_doc)[:, None], jnp.exp(running[count - 1][None, :] - running), 0.0)
        * delta
    )
    weighted = (inputs3.astype(jnp.float32) * to_end[:, :, None]).astype(jnp.bfloat16)
    b_heads = jnp.repeat(b_groups, per_group, axis=1)
    local_state = jnp.einsum("shp,shn->hpn", weighted, b_heads, preferred_element_type=jnp.float32)
    carry_factor = jnp.where(prior_doc == last_doc, jnp.exp(running[count - 1]), 0.0)
    inflow = jnp.where((docs == prior_doc)[:, None], jnp.exp(running), 0.0)
    c_heads = jnp.repeat(c_groups, per_group, axis=1)
    return (intra, local_state, carry_factor, inflow, c_heads)


def stretch_finish(intra, incoming, inflow, c_heads, x_rows, skip_gain, norm_gain):
    count = x_rows.shape[0]
    heads = x_rows.shape[1] // MP
    incoming_bf = incoming.astype(jnp.bfloat16)
    entering = (
        jnp.einsum("thn,hpn->thp", c_heads, incoming_bf, preferred_element_type=jnp.float32)
        * inflow[:, :, None]
    )
    inputs3 = x_rows.reshape(count, heads, MP).astype(jnp.float32)
    mixed = intra + entering + skip_gain[None, :, None] * inputs3
    mean_square = jnp.mean(mixed * mixed, axis=-1, keepdims=True)
    normed = mixed * lax.rsqrt(mean_square + EPS_NORM) * norm_gain.reshape(heads, MP)[None]
    return normed.reshape(count, heads * MP).astype(jnp.bfloat16)


def combine_states(earlier, later):
    return (earlier[0] * later[0], later[0][:, None, None] * earlier[1] + later[1])


def local(
    queries,
    keys,
    values,
    mamba_x,
    mamba_b,
    mamba_c,
    mamba_dt,
    conv_x,
    conv_b,
    conv_c,
    dt_bias,
    decay_rate,
    skip_gain,
    norm_gain,
    windows,
    doc_lengths,
):
    served = (
        lax.all_to_all(queries, "tensor", split_axis=1, concat_axis=0, tiled=True),
        lax.all_to_all(keys, "tensor", split_axis=1, concat_axis=0, tiled=True),
        lax.all_to_all(values, "tensor", split_axis=1, concat_axis=0, tiled=True),
        lax.all_to_all(mamba_x, "tensor", split_axis=1, concat_axis=0, tiled=True),
        lax.all_to_all(mamba_b, "tensor", split_axis=1, concat_axis=0, tiled=True),
        lax.all_to_all(mamba_c, "tensor", split_axis=1, concat_axis=0, tiled=True),
        lax.all_to_all(mamba_dt, "tensor", split_axis=1, concat_axis=0, tiled=True),
    )
    query_rows, key_rows, value_rows, x_rows, b_rows, c_rows, dt_rows = served
    row_count = query_rows.shape[0]
    shard_start = lax.axis_index("seq") * row_count
    positions = shard_start + jnp.arange(row_count, dtype=jnp.int32)
    doc_starts = doc_table(doc_lengths)
    query_heads = query_rows.shape[1] // HEAD_SIZE
    shared_heads = key_rows.shape[1] // HEAD_SIZE
    group_width = query_heads // shared_heads
    window_per_head = lax.dynamic_slice_in_dim(
        windows, lax.axis_index("tensor") * query_heads, query_heads
    ).reshape(shared_heads, group_width)
    reach = jnp.max(window_per_head)
    grouped_heads = query_rows.reshape(row_count, shared_heads, group_width, HEAD_SIZE)
    initial = (
        jnp.full((shared_heads, group_width, row_count), NEG_LARGE, jnp.float32),
        jnp.zeros((shared_heads, group_width, row_count), jnp.float32),
        jnp.zeros((shared_heads, group_width, row_count, HEAD_SIZE), jnp.float32),
    )
    final = attend_piece(
        initial,
        (
            lax.all_gather(key_rows, "seq", axis=0, tiled=True),
            lax.all_gather(value_rows, "seq", axis=0, tiled=True),
        ),
        jnp.int32(0),
        grouped_heads,
        positions,
        doc_starts,
        window_per_head,
        reach,
    )
    final_max, totals, accum = final
    attention = (
        (accum / totals[..., None])
        .transpose(2, 0, 1, 3)
        .reshape(row_count, query_heads * HEAD_SIZE)
        .astype(jnp.bfloat16)
    )
    edge = row_count - (KC - 1)
    tails = shifted((x_rows[edge:], b_rows[edge:], c_rows[edge:]), "seq", 1)
    conv_x_out = causal_conv(
        jnp.concatenate([tails[0], x_rows], axis=0), conv_x, positions, doc_starts
    )
    conv_b_out = causal_conv(
        jnp.concatenate([tails[1], b_rows], axis=0), conv_b, positions, doc_starts
    )
    conv_c_out = causal_conv(
        jnp.concatenate([tails[2], c_rows], axis=0), conv_c, positions, doc_starts
    )
    intra, local_state, carry_factor, inflow, c_heads = stretch_terms(
        conv_x_out, conv_b_out, conv_c_out, dt_rows, positions, doc_starts, dt_bias, decay_rate
    )
    incoming = prefix(
        (carry_factor, local_state),
        "seq",
        combine_states,
        (jnp.ones_like(carry_factor), jnp.zeros_like(local_state)),
    )
    mamba_out = stretch_finish(
        intra, incoming[1], inflow, c_heads, conv_x_out, skip_gain, norm_gain
    )
    sums = lax.psum(
        (
            jnp.sum(attention.astype(jnp.float32), axis=0),
            jnp.sum(mamba_out.astype(jnp.float32), axis=0),
        ),
        "seq",
    )
    return (attention, mamba_out, sums[0], sums[1])


def solution(mesh):
    placed = (
        P(("seq", "tensor"), None),
        P(("seq", "tensor"), None),
        P(("seq", "tensor"), None),
        P(("seq", "tensor"), None),
        P(("seq", "tensor"), None),
        P(("seq", "tensor"), None),
        P(("seq", "tensor"), None),
        P(None, "tensor"),
        P(None, "tensor"),
        P(None, "tensor"),
        P("tensor"),
        P("tensor"),
        P("tensor"),
        P("tensor"),
        P(),
        P(),
    )
    return jax.shard_map(
        local,
        mesh=mesh,
        in_specs=placed,
        out_specs=(P("seq", "tensor"), P("seq", "tensor"), P("tensor"), P("tensor")),
        check_vma=False,
    )
```

profile of v0, /device:TPU:0, one launch (start us, length us, event | category | flops | bytes accessed | tf_op | source)
XLA Modules:
  0.0 185.0 jit_solution(2254786012537562026)
XLA Ops:
  8.7 6.3 %all-to-all-start.4 = ((bf16[4,2,512]{2,1,0:T(2,128)(2,1)}), bf16[4,2,512]{2,1,0:T(2,128)(2,1)S(1)}, u32[]{:S(2)}, u32[]{:S(2)}) async-start(bf16[4,2,512]{2,1,0:T(2,128)(2,1)} %reshape.408), calls=%async_computation.4 | async-start | bytes 16384 | tf_op jit(solution)/shard_map/all_to_all | solution.py:189
  21.0 1.5 copy.168
  22.5 5.1 %all-to-all-start.6 = ((bf16[32,4,256]{2,0,1:T(8,128)(2,1)}), bf16[32,4,256]{2,0,1:T(8,128)(2,1)S(1)}, u32[]{:S(2)}, u32[]{:S(2)}) async-start(bf16[32,4,256]{2,0,1:T(8,128)(2,1)} %bitcast.129), calls=%async_computation.6 | async-start | bytes 131072 | tf_op jit(solution)/shard_map/all_to_all | solution.py:187
  28.1 1.9 %copy.166 = bf16[4,4,8,2048]{3,2,0,1:T(8,128)(2,1)} copy(bf16[4,4,8,2048]{3,2,1,0:T(8,128)(2,1)} %bitcast.155) | data formatting | bytes 1048576 | tf_op jit(solution)/shard_map/all_to_all | solution.py:186
  30.6 2.7 %all-to-all-done.6 = bf16[32,4,256]{2,0,1:T(8,128)(2,1)S(1)} async-done(((bf16[32,4,256]{2,0,1:T(8,128)(2,1)}), bf16[32,4,256]{2,0,1:T(8,128)(2,1)S(1)}, u32[]{:S(2)}, u32[]{:S(2)}) %all-to-all-start.6) | async-done | bytes 65568 | tf_op jit(solution)/shard_map/all_to_all | solution.py:187
  33.3 3.6 %all-to-all-start.3 = ((bf16[32,4,2048]{2,0,1:T(8,128)(2,1)}), bf16[32,4,2048]{2,0,1:T(8,128)(2,1)S(1)}, u32[]{:S(2)}, u32[]{:S(2)}) async-start(bf16[32,4,2048]{2,0,1:T(8,128)(2,1)} %bitcast.127), calls=%async_computation.3 | async-start | bytes 1048576 | tf_op jit(solution)/shard_map/all_to_all | solution.py:186
  41.5 8.2 %all-to-all-done.3 = bf16[32,4,2048]{2,0,1:T(8,128)(2,1)S(1)} async-done(((bf16[32,4,2048]{2,0,1:T(8,128)(2,1)}), bf16[32,4,2048]{2,0,1:T(8,128)(2,1)S(1)}, u32[]{:S(2)}, u32[]{:S(2)}) %all-to-all-start.3) | async-done | bytes 524320 | tf_op jit(solution)/shard_map/all_to_all | solution.py:186
  55.2 3.3 %all-to-all-start.5 = ((bf16[32,4,256]{2,0,1:T(8,128)(2,1)}), bf16[32,4,256]{2,0,1:T(8,128)(2,1)S(1)}, u32[]{:S(2)}, u32[]{:S(2)}) async-start(bf16[32,4,256]{2,0,1:T(8,128)(2,1)} %bitcast.130), calls=%async_computation.5 | async-start | bytes 131072 | tf_op jit(solution)/shard_map/all_to_all | solution.py:188
  61.3 2.9 %all-to-all-done.5 = bf16[32,4,256]{2,0,1:T(8,128)(2,1)S(1)} async-done(((bf16[32,4,256]{2,0,1:T(8,128)(2,1)}), bf16[32,4,256]{2,0,1:T(8,128)(2,1)S(1)}, u32[]{:S(2)}, u32[]{:S(2)}) %all-to-all-start.5) | async-done | bytes 65568 | tf_op jit(solution)/shard_map/all_to_all | solution.py:188
  64.2 3.3 %all-to-all-start = ((bf16[32,4,256]{2,0,1:T(8,128)(2,1)}), bf16[32,4,256]{2,0,1:T(8,128)(2,1)S(1)}, u32[]{:S(2)}, u32[]{:S(2)}) async-start(bf16[32,4,256]{2,0,1:T(8,128)(2,1)} %bitcast.132), calls=%async_computation | async-start | bytes 131072 | tf_op jit(solution)/shard_map/all_to_all | solution.py:184
  70.8 12.8 %all-gather.1 = bf16[8,1,32]{2,1,0:T(2,128)(2,1)S(1)} all-gather(bf16[1,1,32]{2,1,0:T(2,128)(2,1)S(1)} %get-tuple-element.210), channel_id=1, replica_groups=mesh['seq'=8,'tensor'=4] {'seq'}, dimensions={0}, use_global_device_ids=true | all-gather | bytes 576 | tf_op jit(solution)/shard_map/all_gather | solution.py:27
  85.0 2.2 %collective-permute-start.1 = (bf16[3,256]{1,0:T(4,128)(2,1)S(1)}, bf16[3,256]{1,0:T(4,128)(2,1)S(1)}, u32[]{:S(2)}, u32[]{:S(2)}) collective-permute-start(bf16[3,256]{1,0:T(4,128)(2,1)S(1)} %slice.170), channel_id=1, source_target_pairs={{0,4},{4,8},{8,12},{12,16},{16,20},{20,24},{24,28},{1,5},{5,9},{9,... | collective-permute-start | bytes 4616 | tf_op jit(solution)/shard_map/ppermute | solution.py:21
  87.2 5.1 %all-to-all-start.2 = ((bf16[32,4,256]{2,0,1:T(8,128)(2,1)}), bf16[32,4,256]{2,0,1:T(8,128)(2,1)S(1)}, u32[]{:S(2)}, u32[]{:S(2)}) async-start(bf16[32,4,256]{2,0,1:T(8,128)(2,1)} %bitcast.131), calls=%async_computation.2 | async-start | bytes 131072 | tf_op jit(solution)/shard_map/all_to_all | solution.py:185
  92.3 9.3 %all_gather.16 = bf16[1024,256]{1,0:T(8,128)(2,1)S(1)} all-gather(bf16[128,256]{1,0:T(8,128)(2,1)S(1)} %bitcast.162), channel_id=1, replica_groups=mesh['seq'=8,'tensor'=4] {'seq'}, dimensions={0}, use_global_device_ids=true | all-gather | bytes 589824 | tf_op jit(solution)/shard_map/all_gather | solution.py:212
  101.6 4.7 %all-to-all-start.1 = ((bf16[32,4,1024]{2,0,1:T(8,128)(2,1)}), bf16[32,4,1024]{2,0,1:T(8,128)(2,1)S(1)}, u32[]{:S(2)}, u32[]{:S(2)}) async-start(bf16[32,4,1024]{2,0,1:T(8,128)(2,1)} %bitcast.128), calls=%async_computation.1 | async-start | bytes 524288 | tf_op jit(solution)/shard_map/all_to_all | solution.py:183
  106.3 9.7 %all_gather.17 = bf16[1024,256]{1,0:T(8,128)(2,1)S(1)} all-gather(bf16[128,256]{1,0:T(8,128)(2,1)S(1)} %bitcast.163), channel_id=1, replica_groups=mesh['seq'=8,'tensor'=4] {'seq'}, dimensions={0}, use_global_device_ids=true | all-gather | bytes 589824 | tf_op jit(solution)/shard_map/all_gather | solution.py:213
  117.3 1.6 fusion.13
  118.9 13.4 %conditional.1 = (f32[2,4,128]{2,1,0:T(4,128)S(1)}, f32[2,4,128,128]{3,2,1,0:T(8,128)S(1)}) conditional(s32[]{:T(128)} %convert_element_type.180, () %tuple.30, (s32[128]{0:T(128)S(1)}, s32[1024]{0:T(1024)S(1)}, s32[1024]{0:T(1024)S(1)}, s32[3]{0:T(128)S(1)}, s32[1024]{0:T(1024)S(1)}, /*index=5*/s32[8]{0:T(128)}, bf16[1024,256]{1,0:T(8,128)(2,1)S(1)}, ...), branch_computations={%region_2.3_spmd, %region_3.8_spmd} | conditional | flops 557590656 | bytes 36501220 | solution.py:87
  122.0 4.1 %fusion = (f32[2,4,128]{2,1,0:T(4,128)S(1)}, f32[2,1024,128,4]{2,1,3,0:T(8,128)}) fusion(s32[2,4]{1,0:T(2,128)S(1)} %lt.30, s32[128,1024]{0,1:T(8,128)S(1)} %broadcast_subtract_fusion, pred[128,1024]{0,1:T(8,128)(4,1)S(1)} %compare_and_fusion.1, bf16[128,2,4,128]{3,2,1,0:T(4,128)(2,1)S(1)} %reshape.368, bf16[1024,2,128,1]{2,1,0,3:T(2,128)(2,1)} %bitcast.156), kind=kOutput, calls=%fused_computation.3 | convolution fusion | flops 273677312 | bytes 5640224 | tf_op jit(solution)/shard_map/cond/branch_1_fun/tgqd,sgd->gqts/dot_general | solution.py:70
  126.3 4.3 %fusion.1 = f32[2,4,128,128]{3,2,1,0:T(8,128)S(1)} fusion(f32[2,1024,128,4]{2,1,3,0:T(8,128)} %get-tuple-element.206, f32[2,4,128]{2,1,0:T(4,128)S(1)} %broadcast_maximum_fusion, s32[2,4]{1,0:T(2,128)S(1)} %lt.30, s32[128,1024]{0,1:T(8,128)S(1)} %broadcast_subtract_fusion, pred[128,1024]{0,1:T(8,128)(4,1)S(1)} %compare_and_fusion.1, ...), kind=kOutput, calls=%fused_computation.4 | convolution fusion | flops 275775488 | bytes 5902368 | tf_op jit(solution)/shard_map/cond/branch_1_fun/gqts,sgd->gqtd/dot_general | solution.py:78
  130.6 1.6 fusion.3
  133.5 2.0 %convolution_bitcast_fusion.1 = f32[128,32,64]{0,2,1:T(8,128)S(1)} fusion(bf16[128,32,64]{0,2,1:T(8,128)(2,1)S(1)} %bitcast.140, bf16[32,128,128]{2,1,0:T(8,128)(2,1)} %fusion.13), kind=kOutput, calls=%fused_computation.32 | convolution fusion | flops 67108864 | bytes 2621440 | tf_op jit(solution)/shard_map/hts,shp->thp/dot_general | solution.py:130
  135.6 16.0 %while.14 = (s32[]{:T(128)}, f32[32,64,128]{2,1,0:T(8,128)S(1)}, s32[]{:T(128)}, bf16[8,32]{1,0:T(8,128)(2,1)}, bf16[8,32,64,128]{3,2,1,0:T(8,128)(2,1)}, /*index=5*/s32[]{:T(128)}, s32[]{:T(128)}) while((s32[]{:T(128)}, f32[32,64,128]{2,1,0:T(8,128)S(1)}, s32[]{:T(128)}, bf16[8,32]{1,0:T(8,128)(2,1)}, ...), condition=%wide.region_13.14_spmd.clone, body=%wide.region_12.13_spmd.clone.sunk | while | flops 1310756 | bytes 2621865 | solution.py:40
  154.6 23.6 %all-reduce = (f32[1024]{0:T(1024)}, f32[2048]{0:T(1024)}) all-reduce(f32[1024]{0:T(1024)S(1)} %bitcast.175, f32[2048]{0:T(1024)S(1)} %reduce_sum.112), channel_id=1, replica_groups=mesh['seq'=8,'tensor'=4] {'seq'}, use_global_device_ids=true, to_apply=%region_16.17 | all-reduce | flops 3072 | bytes 24576 | tf_op jit(solution)/shard_map/psum | solution.py:252
  (123 shorter events, 46.0 us)
Async XLA Ops:
  8.7 13.8 %all-to-all-start.4 = ((bf16[4,2,512]{2,1,0:T(2,128)(2,1)}), bf16[4,2,512]{2,1,0:T(2,128)(2,1)S(1)}, u32[]{:S(2)}, u32[]{:S(2)}) async-start(bf16[4,2,512]{2,1,0:T(2,128)(2,1)} %reshape.408), calls=%async_computation.4 | async-start | bytes 16384 | tf_op jit(solution)/shard_map/all_to_all | solution.py:189
  22.5 10.8 %all-to-all-start.6 = ((bf16[32,4,256]{2,0,1:T(8,128)(2,1)}), bf16[32,4,256]{2,0,1:T(8,128)(2,1)S(1)}, u32[]{:S(2)}, u32[]{:S(2)}) async-start(bf16[32,4,256]{2,0,1:T(8,128)(2,1)} %bitcast.129), calls=%async_computation.6 | async-start | bytes 131072 | tf_op jit(solution)/shard_map/all_to_all | solution.py:187
  30.0 24.6 %copy-start.5 = (bf16[32,1024]{1,0:T(8,128)(2,1)S(1)}, bf16[32,1024]{1,0:T(8,128)(2,1)}, u32[]{:S(2)}) copy-start(bf16[32,1024]{1,0:T(8,128)(2,1)} %param.25) | copy-start | bytes 196612
  33.3 25.3 %copy-start.9 = (bf16[4,256]{1,0:T(4,128)(2,1)S(1)}, bf16[4,256]{1,0:T(4,128)(2,1)}, u32[]{:S(2)}) copy-start(bf16[4,256]{1,0:T(4,128)(2,1)} %param.29) | copy-start | bytes 6148
  33.3 25.3 %copy-start.8 = (f32[2048]{0:T(1024)S(1)}, f32[2048]{0:T(1024)}, u32[]{:S(2)}) copy-start(f32[2048]{0:T(1024)} %param.33) | copy-start | bytes 24580
  33.3 26.0 %copy-start.6 = (bf16[32,1024]{1,0:T(8,128)(2,1)S(1)}, bf16[32,1024]{1,0:T(8,128)(2,1)}, u32[]{:S(2)}) copy-start(bf16[32,1024]{1,0:T(8,128)(2,1)} %param.21) | copy-start | bytes 196612
  33.3 26.6 %copy-start.7 = (bf16[32,1024]{1,0:T(8,128)(2,1)S(1)}, bf16[32,1024]{1,0:T(8,128)(2,1)}, u32[]{:S(2)}) copy-start(bf16[32,1024]{1,0:T(8,128)(2,1)} %param.22) | copy-start | bytes 196612
  33.3 27.2 %copy-start.2 = (bf16[32,4096]{1,0:T(8,128)(2,1)S(1)}, bf16[32,4096]{1,0:T(8,128)(2,1)}, u32[]{:S(2)}) copy-start(bf16[32,4096]{1,0:T(8,128)(2,1)} %param.20) | copy-start | bytes 786436
  33.3 16.4 %all-to-all-start.3 = ((bf16[32,4,2048]{2,0,1:T(8,128)(2,1)}), bf16[32,4,2048]{2,0,1:T(8,128)(2,1)S(1)}, u32[]{:S(2)}, u32[]{:S(2)}) async-start(bf16[32,4,2048]{2,0,1:T(8,128)(2,1)} %bitcast.127), calls=%async_computation.3 | async-start | bytes 1048576 | tf_op jit(solution)/shard_map/all_to_all | solution.py:186
  36.9 30.6 %copy-start.11 = (s32[32]{0:T(128)S(1)}, s32[32]{0:T(128)}, u32[]{:S(2)}) copy-start(s32[32]{0:T(128)} %param.34) | copy-start | bytes 388
  37.0 98.6 %all-gather.4.cloned.1.call-start = ((), (), s32[]{:S(2)}) async-start(), calls=%async_computation.7 | async-start | bytes 4718592 | tf_op jit(solution)/shard_map/all_gather | solution.py:27
  39.4 11.6 %collective-permute-start.2 = (bf16[3,256]{1,0:T(4,128)(2,1)S(1)}, bf16[3,256]{1,0:T(4,128)(2,1)S(1)}, u32[]{:S(2)}, u32[]{:S(2)}) collective-permute-start(bf16[3,256]{1,0:T(4,128)(2,1)S(1)} %slice.175), channel_id=1, source_target_pairs={{0,4},{4,8},{8,12},{12,16},{16,20},{20,24},{24,28},{1,5},{5,9},{9,... | collective-permute-start | bytes 4616 | tf_op jit(solution)/shard_map/ppermute | solution.py:21
  49.7 2.1 %collective-permute-start = (bf16[3,2048]{1,0:T(4,128)(2,1)S(1)}, bf16[3,2048]{1,0:T(4,128)(2,1)S(1)}, u32[]{:S(2)}, u32[]{:S(2)}) collective-permute-start(bf16[3,2048]{1,0:T(4,128)(2,1)S(1)} %slice.165), channel_id=1, source_target_pairs={{0,4},{4,8},{8,12},{12,16},{16,20},{20,24},{24,28},{1,5},{5,9},{9,... | collective-permute-start | bytes 36872 | tf_op jit(solution)/shard_map/ppermute | solution.py:21
  55.2 9.0 %all-to-all-start.5 = ((bf16[32,4,256]{2,0,1:T(8,128)(2,1)}), bf16[32,4,256]{2,0,1:T(8,128)(2,1)S(1)}, u32[]{:S(2)}, u32[]{:S(2)}) async-start(bf16[32,4,256]{2,0,1:T(8,128)(2,1)} %bitcast.130), calls=%async_computation.5 | async-start | bytes 131072 | tf_op jit(solution)/shard_map/all_to_all | solution.py:188
  64.2 23.0 %all-to-all-start = ((bf16[32,4,256]{2,0,1:T(8,128)(2,1)}), bf16[32,4,256]{2,0,1:T(8,128)(2,1)S(1)}, u32[]{:S(2)}, u32[]{:S(2)}) async-start(bf16[32,4,256]{2,0,1:T(8,128)(2,1)} %bitcast.132), calls=%async_computation | async-start | bytes 131072 | tf_op jit(solution)/shard_map/all_to_all | solution.py:184
  85.0 31.1 %collective-permute-start.1 = (bf16[3,256]{1,0:T(4,128)(2,1)S(1)}, bf16[3,256]{1,0:T(4,128)(2,1)S(1)}, u32[]{:S(2)}, u32[]{:S(2)}) collective-permute-start(bf16[3,256]{1,0:T(4,128)(2,1)S(1)} %slice.170), channel_id=1, source_target_pairs={{0,4},{4,8},{8,12},{12,16},{16,20},{20,24},{24,28},{1,5},{5,9},{9,... | collective-permute-start | bytes 4616 | tf_op jit(solution)/shard_map/ppermute | solution.py:21
  87.2 14.4 %all-to-all-start.2 = ((bf16[32,4,256]{2,0,1:T(8,128)(2,1)}), bf16[32,4,256]{2,0,1:T(8,128)(2,1)S(1)}, u32[]{:S(2)}, u32[]{:S(2)}) async-start(bf16[32,4,256]{2,0,1:T(8,128)(2,1)} %bitcast.131), calls=%async_computation.2 | async-start | bytes 131072 | tf_op jit(solution)/shard_map/all_to_all | solution.py:185
  101.6 17.3 %all-to-all-start.1 = ((bf16[32,4,1024]{2,0,1:T(8,128)(2,1)}), bf16[32,4,1024]{2,0,1:T(8,128)(2,1)S(1)}, u32[]{:S(2)}, u32[]{:S(2)}) async-start(bf16[32,4,1024]{2,0,1:T(8,128)(2,1)} %bitcast.128), calls=%async_computation.1 | async-start | bytes 524288 | tf_op jit(solution)/shard_map/all_to_all | solution.py:183
  126.3 4.4 %copy-start = (f32[2,1024,128,4]{2,1,3,0:T(8,128)S(1)}, f32[2,1024,128,4]{2,1,3,0:T(8,128)}, u32[]{:S(2)}) copy-start(f32[2,1024,128,4]{2,1,3,0:T(8,128)} %get-tuple-element.206) | copy-start | bytes 12582916 | tf_op jit(solution)/shard_map/cond
  135.6 16.1 %copy-start.1 = (bf16[128,2,128]{2,0,1:T(8,128)(2,1)S(1)}, bf16[128,2,128]{2,0,1:T(8,128)(2,1)}, u32[]{:S(2)}) copy-start(bf16[128,2,128]{2,0,1:T(8,128)(2,1)} %copy.129) | copy-start | bytes 196612
  135.6 16.3 %copy-start.3 = (f32[128,32]{0,1:T(8,128)S(1)}, f32[128,32]{0,1:T(8,128)}, u32[]{:S(2)}) copy-start(f32[128,32]{0,1:T(8,128)} %copy.130) | copy-start | bytes 49156
  135.6 16.3 %copy-start.10 = (f32[32]{0:T(128)S(1)}, f32[32]{0:T(128)}, u32[]{:S(2)}) copy-start(f32[32]{0:T(128)} %param.32) | copy-start | bytes 388
  151.7 1.2 copy-start.4
Sparse Core Ops, SparseCore 0:
  54.7 38.6 all-gather.3
where the time goes:
time: 187 us; the launch traced here: 185 us
  blocking collectives  55.4 us (30%)
  starting transfers between devices  36.3 us (19%)
  other arithmetic  30.3 us (16%)
  between operations  19 us (10%)
  local copies, waits for them, and re-layouts  16.8 us (9%)
  waiting for transfers between devices  14.2 us (8%)
  matrix products  12.8 us (7%)
    psum x1, blocking collectives, local(): lax.psum((jnp.sum(attention.astype(jnp.float32), axis=0), jnp.sum(mamba_o...  23.6 us
    all_gather x1, blocking collectives, prefix(): lax.all_gather(part.astype(kind), axis)  12.8 us
    select_n x8, other arithmetic, turn(): return jax.tree.map(lambda a, b: jnp.where(reached, a, b), new, before)  10.4 us
    all_gather x1, blocking collectives, local(): lax.all_gather(value_rows, 'seq', axis=0, tiled=True)  9.74 us
    all_gather x1, blocking collectives, local(): lax.all_gather(key_rows, 'seq', axis=0, tiled=True)  9.29 us
    all_to_all x1, waiting for transfers between devices, local(): lax.all_to_all(mamba_x, 'tensor', split_axis=1, concat_axis=0, tiled=True)  8.17 us
    all_to_all x1, starting transfers between devices, local(): lax.all_to_all(mamba_dt, 'tensor', split_axis=1, concat_axis=0, tiled=True)  6.35 us
    convert_element_type x8, other arithmetic, turn(): part[k].astype(own.dtype)  5.54 us
  transfers between devices with their start and end apart: 11, of which 4 were waited for; matrix products, arithmetic and copies ran while one was open for 20% of the time, Pallas kernels for 0%

commit v1 on v0

v1 whole, which is shorter than its diff:
```python
import functools
import math

import jax
import jax.numpy as jnp
from jax import lax
from jax.experimental import pallas as pl
from jax.experimental.pallas import tpu as pltpu
from jax.sharding import PartitionSpec as P

HEAD_SIZE = 128
MP = 64
MN = 128
KC = 4
TAIL = 16
LANES = 128

NEG_LARGE = -1e30
EPS_NORM = 1e-05
F32 = jnp.float32
BF16 = jnp.bfloat16


def parts3(v):
    a = v.astype(BF16)
    r = v - a.astype(F32)
    b = r.astype(BF16)
    c = (r - b.astype(F32)).astype(BF16)
    return a, b, c


def mm(a, b):
    return jnp.dot(a, b, preferred_element_type=F32)


def mm_t(a, b):
    return lax.dot_general(a, b, (((1,), (1,)), ((), ())), preferred_element_type=F32)


def iota(shape, dim):
    return lax.broadcasted_iota(jnp.int32, shape, dim)


def doc_of(pos, starts):
    total = jnp.full(pos.shape, -1, jnp.int32)
    for s in starts:
        total = total + (pos >= s).astype(jnp.int32)
    return total


def rdma(src, dst, send, recv, axis, peer):
    return pltpu.make_async_remote_copy(
        src_ref=src,
        dst_ref=dst,
        send_sem=send,
        recv_sem=recv,
        device_id={axis: peer},
        device_id_type=pl.DeviceIdType.MESH,
    )


def kernel(
    S,
    T,
    q_in,
    k_in,
    v_in,
    x_in,
    b_in,
    c_in,
    dt_in,
    conv_x,
    conv_b,
    conv_c,
    bias_ref,
    decay_ref,
    gain_ref,
    skip_ref,
    windows_ref,
    doclen_ref,
    attn_ref,
    mamba_ref,
    asum_ref,
    msum_ref,
    qbuf,
    kv,
    xbc,
    dtbuf,
    xc,
    bcbuf,
    full,
    inflow_ref,
    gapbuf,
    colbuf,
    cumt,
    deltat,
    crossm,
    state,
    gstate,
    fac,
    gfac,
    fexp,
    ret,
    incf,
    incoming,
    sums,
    a_send,
    a_recv,
    kv_send,
    kv_recv,
    tail_sem,
    st_send,
    st_recv,
    f_send,
    f_recv,
    r_send,
    r_recv,
    c_send,
    c_recv,
):
    me = lax.axis_index("seq")
    mt = lax.axis_index("tensor")
    piece = q_in.shape[0]
    rows = piece * T
    qw, kw, xw = q_in.shape[1] // T, k_in.shape[1] // T, x_in.shape[1] // T
    bw = b_in.shape[1] // T
    heads = xw // MP
    groups = bw // MN
    per_group = heads // groups
    qheads = qw // HEAD_SIZE
    holders = gstate.shape[0] and state.shape[0] // gstate.shape[1]
    stride = S // holders
    srows = gstate.shape[1]

    barrier = pltpu.get_barrier_semaphore()
    for d in range(1, T):
        pl.semaphore_signal(
            barrier, inc=1, device_id={"tensor": lax.rem(mt + d, T)},
            device_id_type=pl.DeviceIdType.MESH,
        )

    def greet(d, carry):
        pl.semaphore_signal(
            barrier, inc=1, device_id={"seq": lax.rem(me + d, S)},
            device_id_type=pl.DeviceIdType.MESH,
        )
        return carry

    lax.fori_loop(1, S, greet, 0)
    pl.semaphore_wait(barrier, T - 1 + S - 1)

    base = me * rows

    def dst_of(a, source):
        if a == 0:
            return kv.at[pl.ds(pl.multiple_of(base + source * piece, piece), piece), pl.ds(0, kw)]
        if a == 1:
            return kv.at[pl.ds(pl.multiple_of(base + source * piece, piece), piece), pl.ds(kw, kw)]
        ext = pl.ds(pl.multiple_of(TAIL + source * piece, TAIL), piece)
        if a == 2:
            return dtbuf.at[pl.ds(pl.multiple_of(source * piece, piece), piece), :]
        if a == 3:
            return xbc.at[ext, pl.ds(xw, bw)]
        if a == 4:
            return xbc.at[ext, pl.ds(xw + bw, bw)]
        if a == 5:
            return xbc.at[ext, pl.ds(0, xw)]
        return qbuf.at[pl.ds(pl.multiple_of(source * piece, piece), piece), :]

    ins = (k_in, v_in, dt_in, b_in, c_in, x_in, q_in)
    widths = (kw, kw, None, bw, bw, xw, qw)

    def src_of(a, target):
        if widths[a] is None:
            return ins[a].at[:, :]
        w = widths[a]
        return ins[a].at[:, pl.ds(pl.multiple_of(target * w, w), w)]

    def a2a_send(a, d):
        target = lax.rem(mt + d, T)
        return rdma(src_of(a, target), dst_of(a, mt), a_send.at[a, d], a_recv.at[a, d], "tensor", target)

    def a2a_local(a):
        return pltpu.make_async_copy(src_of(a, mt), dst_of(a, mt), a_recv.at[a, 0])

    def a2a_wait(a):
        a2a_local(a).wait()
        for d in range(1, T):
            source = lax.rem(mt + T - d, T)
            rdma(
                src_of(a, mt), dst_of(a, source), a_send.at[a, d], a_recv.at[a, d], "tensor", source
            ).wait_recv()

    for a in range(7):
        for d in range(1, T):
            a2a_send(a, d).start()
        a2a_local(a).start()

    starts = []
    running = jnp.int32(0)
    for i in range(doclen_ref.shape[0]):
        starts.append(running)
        running = running + doclen_ref[i]

    keys = S * rows
    key_chunk = min(keys, 1024)
    n_chunks = keys // key_chunk

    def gap_chunk(c, carry):
        t = base + iota((rows, key_chunk), 0)
        s = c * key_chunk + iota((rows, key_chunk), 1)
        dq = doc_of(base + iota((rows, 1), 0), starts)
        dk = doc_of(c * key_chunk + iota((1, key_chunk), 1), starts)
        gap = t - s
        ok = (gap >= 0) & (dq == dk)
        gapbuf[:, pl.ds(pl.multiple_of(c * key_chunk, key_chunk), key_chunk)] = jnp.where(
            ok, gap, jnp.int32(1 << 30)
        )
        return carry

    lax.fori_loop(0, n_chunks, gap_chunk, 0)

    a2a_wait(0)
    a2a_wait(1)

    def kv_block(owner):
        return kv.at[pl.ds(pl.multiple_of(owner * rows, rows), rows), :]

    def kv_copy(d, owner, peer):
        return rdma(kv_block(owner), kv_block(owner), kv_send.at[d], kv_recv.at[d], "seq", peer)

    def kv_start(d, carry):
        kv_copy(d, me, lax.rem(me + d, S)).start()
        return carry

    lax.fori_loop(1, S, kv_start, 0)

    a2a_wait(2)
    hot = (iota((LANES, heads), 0) == iota((LANES, heads), 1) + mt * heads).astype(BF16)
    dt = mm(dtbuf[...], hot)
    v = dt + bias_ref[...]
    delta = jnp.maximum(v, 0.0) + jnp.log1p(jnp.exp(-jnp.abs(v)))
    logd = -delta * decay_ref[...]
    lower = (iota((rows, rows), 0) >= iota((rows, rows), 1)).astype(BF16)
    cum = sum(mm(lower, p) for p in parts3(logd))
    eye = (iota((heads, heads), 0) == iota((heads, heads), 1)).astype(BF16)
    cumt[...] = sum(mm_t(eye, p) for p in parts3(cum))
    deltat[...] = sum(mm_t(eye, p) for p in parts3(delta))
    for i in range(heads // 2):
        colbuf[i, :, :] = cum[:, 2 * i : 2 * i + 2]
    docs = doc_of(base + iota((rows, 1), 0), starts)
    docs_row = doc_of(base + iota((1, rows), 1), starts)
    last_doc = doc_of(base + rows - 1 + jnp.zeros((1, 1), jnp.int32), starts)
    prior_doc = doc_of(base - 1 + jnp.zeros((1, 1), jnp.int32), starts)
    ending = cum[rows - 1 : rows, :]
    to_end = jnp.where(docs == last_doc, jnp.exp(ending - cum), 0.0) * delta
    factor = jnp.where(prior_doc == last_doc, jnp.exp(ending), 0.0)
    fac[...] = jnp.broadcast_to(factor, fac.shape)
    inflow = jnp.where(docs == prior_doc, jnp.exp(cum), 0.0)
    te = parts3(to_end)
    inf = parts3(inflow)

    a2a_wait(3)
    a2a_wait(4)
    a2a_wait(5)

    def tail_copy(peer):
        return rdma(
            xbc.at[pl.ds(rows, TAIL), :], xbc.at[pl.ds(0, TAIL), :],
            tail_sem.at[0], tail_sem.at[1], "seq", peer,
        )

    @pl.when(me < S - 1)
    def _():
        tail_copy(lax.rem(me + 1, S)).start()

    @pl.when(me > 0)
    def _():
        tail_copy(lax.rem(me + S - 1, S)).wait_recv()

    @pl.when(me == 0)
    def _():
        xbc[pl.ds(0, TAIL), :] = jnp.zeros((TAIL, xbc.shape[1]), BF16)

    width = 256 if xw % 256 == 0 and bw % 256 == 0 else 128
    pos = base + iota((rows, 1), 0)
    keeps = []
    for j in range(KC):
        same = (doc_of(pos - j, starts) == docs) & (pos - j >= 0)
        keeps.append(jnp.broadcast_to(same.astype(F32), (rows, width)))

    def conv(lane, taps, tap_lane):
        xe = xbc[:, pl.ds(lane, width)].astype(F32)
        tp = taps[:, pl.ds(tap_lane, width)].astype(F32)
        u = tp[0:1] * xe[TAIL : TAIL + rows]
        for j in range(1, KC):
            u = u + (tp[j : j + 1] * xe[TAIL - j : TAIL - j + rows]) * keeps[j]
        return (u / (1.0 + jnp.exp(-u))).astype(BF16)

    for i in range(bw // width):
        bcbuf[:, i * width : (i + 1) * width] = conv(xw + i * width, conv_b, i * width)
        bcbuf[:, bw + i * width : bw + (i + 1) * width] = conv(
            xw + bw + i * width, conv_c, i * width
        )

    causal = (iota((rows, rows), 0) >= iota((rows, rows), 1)) & (docs == docs_row)
    for g in range(groups):
        bg = bcbuf[:, g * MN : (g + 1) * MN]
        cg = bcbuf[:, bw + g * MN : bw + (g + 1) * MN]
        crossm[g] = jnp.where(causal, mm_t(cg, bg), 0.0)

    for g in range(groups):
        bt = bcbuf[:, g * MN : (g + 1) * MN].astype(F32).T.astype(BF16)
        gw = per_group * MP

        def stretch(i, carry, g=g, gw=gw, bt=bt):
            lane = pl.multiple_of(g * gw + i * width, width)
            out = conv(lane, conv_x, lane)
            xc[:, pl.ds(lane, width)] = out
            spread = (
                iota((heads, width), 0) == (lane + iota((heads, width), 1)) // MP
            ).astype(BF16)
            to_end_x = mm(te[0], spread) + mm(te[1], spread) + mm(te[2], spread)
            inflow_ref[:, pl.ds(lane, width)] = (
                mm(inf[0], spread) + mm(inf[1], spread) + mm(inf[2], spread)
            )
            weighted = (to_end_x * out.astype(F32)).astype(BF16)
            state[:, pl.ds(lane, width)] = mm(bt, weighted).astype(BF16)
            return carry

        lax.fori_loop(0, gw // width, stretch, 0)

    def st_copy(d, holder, owner, peer):
        return rdma(
            state.at[pl.ds(pl.multiple_of(holder * srows, srows), srows), :],
            gstate.at[owner], st_send.at[d], st_recv.at[d], "seq", peer,
        )

    def f_copy(d, owner, peer):
        return rdma(fac, gfac.at[owner], f_send.at[d], f_recv.at[d], "seq", peer)

    def st_local():
        return pltpu.make_async_copy(
            state.at[pl.ds(pl.multiple_of((me // stride) * srows, srows), srows), :],
            gstate.at[me], st_recv.at[0],
        )

    def st_start(d, carry):
        peer = lax.rem(me + d, S)

        @pl.when(lax.rem(peer, stride) == 0)
        def _():
            st_copy(d, peer // stride, me, peer).start()
            f_copy(d, me, peer).start()

        return carry

    lax.fori_loop(1, S, st_start, 0)
    is_holder = lax.rem(me, stride) == 0

    @pl.when(is_holder)
    def _():
        st_local().start()
        gfac[me] = fac[...]

    half = iota((1, 2 * MP), 1) < MP

    def intra(i, carry):
        lane = pl.multiple_of(i * 2 * MP, 2 * MP)
        cols = colbuf[i]
        cross = crossm[(2 * i) // per_group]
        mixes = []
        for k in range(2):
            gap = cols[:, k : k + 1] - cumt[pl.ds(2 * i + k, 1), :]
            w = jnp.exp(jnp.minimum(gap, 0.0)) * deltat[pl.ds(2 * i + k, 1), :]
            mixes.append((w * cross).astype(BF16))
        xp = xc[:, pl.ds(lane, 2 * MP)]
        zero = jnp.zeros_like(xp)
        halves = jnp.broadcast_to(half, xp.shape)
        stacked = jnp.concatenate(
            [jnp.where(halves, xp, zero), jnp.where(halves, zero, xp)], axis=0
        )
        skip = jnp.where(half, skip_ref[2 * i], skip_ref[2 * i + 1])
        full[:, pl.ds(lane, 2 * MP)] = (
            mm(jnp.concatenate(mixes, axis=1), stacked) + skip * xp.astype(F32)
        )
        return carry

    lax.fori_loop(0, heads // 2, intra, 0)

    def ret_copy(d, target, holder, peer):
        return rdma(
            ret.at[target],
            incoming.at[pl.ds(pl.multiple_of(holder * srows, srows), srows), :],
            r_send.at[d], r_recv.at[d], "seq", peer,
        )

    def ret_local():
        return pltpu.make_async_copy(
            ret.at[me],
            incoming.at[pl.ds(pl.multiple_of((me // stride) * srows, srows), srows), :],
            r_recv.at[0],
        )

    @pl.when(is_holder)
    def _():
        st_local().wait()

        def arrive(d, carry):
            owner = lax.rem(me + S - d, S)
            st_copy(d, me // stride, owner, owner).wait_recv()
            f_copy(d, owner, owner).wait_recv()
            return carry

        lax.fori_loop(1, S, arrive, 0)
        spread = (iota((heads, xw), 0) == iota((heads, xw), 1) // MP).astype(BF16)
        fp = parts3(gfac[...].reshape(S * 8, heads))
        fexp[...] = (mm(fp[0], spread) + mm(fp[1], spread) + mm(fp[2], spread)).reshape(
            S, 8, xw
        )
        incf[...] = jnp.zeros_like(incf)

        def scan(k, carry):
            now = incf[...]
            ret[k] = now.astype(BF16)
            incf[...] = fexp[k][0:1, :] * now + gstate[k].astype(F32)
            return carry

        lax.fori_loop(0, S, scan, 0)
        ret_local().start()

        def give(d, carry):
            peer = lax.rem(me + d, S)
            ret_copy(d, peer, me // stride, peer).start()
            return carry

        lax.fori_loop(1, S, give, 0)

    a2a_wait(6)

    def kv_wait(d, carry):
        owner = lax.rem(me + S - d, S)
        kv_copy(d, owner, owner).wait_recv()
        return carry

    lax.fori_loop(1, S, kv_wait, 0)

    to_exp2 = math.log2(math.e) / math.sqrt(HEAD_SIZE)
    width_of_group = qheads // (kw // HEAD_SIZE)

    def attend(i, carry):
        lane = pl.multiple_of(i * 2 * HEAD_SIZE, 2 * HEAD_SIZE)
        q2 = jnp.concatenate(
            [qbuf[:, pl.ds(lane, HEAD_SIZE)],
             qbuf[:, pl.ds(pl.multiple_of(lane + HEAD_SIZE, HEAD_SIZE), HEAD_SIZE)]], axis=0
        )
        g = (2 * i) // width_of_group
        klane = pl.multiple_of(g * HEAD_SIZE, HEAD_SIZE)
        vlane = pl.multiple_of(kw + g * HEAD_SIZE, HEAD_SIZE)
        wins = [windows_ref[mt * qheads + 2 * i + k] for k in range(2)]

        def piece_of(c, old):
            ks = pl.ds(pl.multiple_of(c * key_chunk, key_chunk), key_chunk)
            s = mm_t(q2, kv[ks, pl.ds(klane, HEAD_SIZE)])
            gap = gapbuf[:, ks]
            s = jnp.concatenate(
                [jnp.where(gap < wins[k], s[k * rows : (k + 1) * rows], NEG_LARGE)
                 for k in range(2)], axis=0
            )
            top = jnp.max(s, axis=1, keepdims=True)
            if old is not None:
                top = jnp.maximum(top, old[0])
            w = jnp.exp2((s - top) * to_exp2)
            total = jnp.sum(w, axis=1, keepdims=True)
            acc = mm(w.astype(BF16), kv[ks, pl.ds(vlane, HEAD_SIZE)])
            if old is not None:
                shrink = jnp.exp2((old[0] - top) * to_exp2)
                total = total + shrink * old[1]
                acc = acc + shrink * old[2]
            return top, total, acc

        if n_chunks == 1:
            top, total, acc = piece_of(0, None)
        else:
            top, total, acc = lax.fori_loop(
                0, n_chunks, piece_of,
                (jnp.full((2 * rows, 1), NEG_LARGE, F32), jnp.zeros((2 * rows, 1), F32),
                 jnp.zeros((2 * rows, HEAD_SIZE), F32)),
            )
        out = (acc / total).astype(BF16)
        for k in range(2):
            o = out[k * rows : (k + 1) * rows]
            at = pl.ds(pl.multiple_of(lane + k * HEAD_SIZE, HEAD_SIZE), HEAD_SIZE)
            attn_ref[:, at] = o
            sums[me, :, at] = jnp.sum(o.astype(F32), axis=0, keepdims=True)
        return carry

    lax.fori_loop(0, qheads // 2, attend, 0)

    def collect(h, carry):
        @pl.when(h * stride != me)
        def _():
            peer = h * stride
            d = lax.rem(me - peer + S, S)
            ret_copy(d, me, h, peer).wait_recv()

        return carry

    lax.fori_loop(0, holders, collect, 0)

    @pl.when(is_holder)
    def _():
        ret_local().wait()

    pair = 2 * MP
    ones = (iota((pair, pair), 0) // MP == iota((pair, pair), 1) // MP).astype(BF16)

    def finish(i, carry):
        lane = pl.multiple_of(i * pair, pair)
        g = (2 * i) // per_group
        cg = bcbuf[:, pl.ds(pl.multiple_of(bw + g * MN, MN), MN)]
        entering = mm(cg, incoming[:, pl.ds(lane, pair)])
        y = full[:, pl.ds(lane, pair)] + entering * inflow_ref[:, pl.ds(lane, pair)]
        p = parts3(y * y)
        mean = (mm(p[0], ones) + mm(p[1], ones) + mm(p[2], ones)) * (1.0 / MP)
        o = (y * lax.rsqrt(mean + EPS_NORM) * gain_ref[:, pl.ds(lane, pair)]).astype(BF16)
        mamba_ref[:, pl.ds(lane, pair)] = o
        sums[me, :, pl.ds(pl.multiple_of(qw + lane, pair), pair)] = jnp.sum(
            o.astype(F32), axis=0, keepdims=True
        )
        return carry

    lax.fori_loop(0, heads // 2, finish, 0)

    def sum_copy(d, owner, peer):
        return rdma(sums.at[owner], sums.at[owner], c_send.at[d], c_recv.at[d], "seq", peer)

    def sum_start(d, carry):
        sum_copy(d, me, lax.rem(me + d, S)).start()
        return carry

    lax.fori_loop(1, S, sum_start, 0)

    for a in range(7):
        for d in range(1, T):
            a2a_send(a, d).wait_send()

    @pl.when(me < S - 1)
    def _():
        tail_copy(lax.rem(me + 1, S)).wait_send()

    def drain(d, carry):
        peer = lax.rem(me + d, S)
        kv_copy(d, me, peer).wait_send()

        @pl.when(lax.rem(peer, stride) == 0)
        def _():
            st_copy(d, peer // stride, me, peer).wait_send()
            f_copy(d, me, peer).wait_send()

        @pl.when(is_holder)
        def _():
            ret_copy(d, peer, me // stride, peer).wait_send()

        return carry

    lax.fori_loop(1, S, drain, 0)

    def sum_wait(d, carry):
        owner = lax.rem(me + S - d, S)
        sum_copy(d, owner, owner).wait_recv()
        sum_copy(d, me, lax.rem(me + d, S)).wait_send()
        return carry

    lax.fori_loop(1, S, sum_wait, 0)

    def add(k, total):
        return total + sums[k]

    total = lax.fori_loop(0, S, add, jnp.zeros((1, sums.shape[2]), F32))
    asum_ref[...] = total[:, :qw]
    msum_ref[...] = total[:, qw:]


def local(
    S,
    T,
    queries,
    keys,
    values,
    mamba_x,
    mamba_b,
    mamba_c,
    mamba_dt,
    conv_x,
    conv_b,
    conv_c,
    dt_bias,
    decay_rate,
    skip_gain,
    norm_gain,
    windows,
    doc_lengths,
):
    rows = queries.shape[0] * T
    qw, kw, xw, bw = (a.shape[1] // T for a in (queries, keys, mamba_x, mamba_b))
    heads = xw // MP
    holders = min(S, MN // 16)
    srows = MN // holders
    vmem = pl.BlockSpec(memory_space=pltpu.VMEM)
    smem = pl.BlockSpec(memory_space=pltpu.SMEM)
    dma = pltpu.SemaphoreType.DMA
    attn, mamba, asum, msum = pl.pallas_call(
        functools.partial(kernel, S, T),
        out_shape=(
            jax.ShapeDtypeStruct((rows, qw), BF16),
            jax.ShapeDtypeStruct((rows, xw), BF16),
            jax.ShapeDtypeStruct((1, qw), F32),
            jax.ShapeDtypeStruct((1, xw), F32),
        ),
        in_specs=[vmem] * 13 + [smem] * 3,
        out_specs=(vmem,) * 4,
        scratch_shapes=[
            pltpu.VMEM((rows, qw), BF16),
            pltpu.VMEM((S * rows, 2 * kw), BF16),
            pltpu.VMEM((TAIL + rows, xw + 2 * bw), BF16),
            pltpu.VMEM((rows, mamba_dt.shape[1]), BF16),
            pltpu.VMEM((rows, xw), BF16),
            pltpu.VMEM((rows, 2 * bw), BF16),
            pltpu.VMEM((rows, xw), F32),
            pltpu.VMEM((rows, xw), F32),
            pltpu.VMEM((rows, S * rows), jnp.int32),
            pltpu.VMEM((heads // 2, rows, 2), F32),
            pltpu.VMEM((heads, rows), F32),
            pltpu.VMEM((heads, rows), F32),
            pltpu.VMEM((bw // MN, rows, rows), F32),
            pltpu.VMEM((MN, xw), BF16),
            pltpu.VMEM((S, srows, xw), BF16),
            pltpu.VMEM((8, heads), F32),
            pltpu.VMEM((S, 8, heads), F32),
            pltpu.VMEM((S, 8, xw), F32),
            pltpu.VMEM((S, srows, xw), BF16),
            pltpu.VMEM((srows, xw), F32),
            pltpu.VMEM((MN, xw), BF16),
            pltpu.VMEM((S, 1, qw + xw), F32),
            dma((7, T)),
            dma((7, T)),
            dma((S,)),
            dma((S,)),
            dma((2,)),
            dma((S,)),
            dma((S,)),
            dma((S,)),
            dma((S,)),
            dma((S,)),
            dma((S,)),
            dma((S,)),
            dma((S,)),
        ],
        compiler_params=pltpu.CompilerParams(
            collective_id=0, has_side_effects=True, vmem_limit_bytes=60 * 1024 * 1024
        ),
    )(
        queries, keys, values, mamba_x, mamba_b, mamba_c, mamba_dt, conv_x, conv_b, conv_c,
        dt_bias.reshape(1, -1), decay_rate.reshape(1, -1), norm_gain.reshape(1, -1),
        skip_gain, windows, doc_lengths,
    )
    return attn, mamba, asum.reshape(-1), msum.reshape(-1)


def solution(mesh):
    rows = P(("seq", "tensor"), None)
    return jax.shard_map(
        functools.partial(local, mesh.shape["seq"], mesh.shape["tensor"]),
        mesh=mesh,
        in_specs=(rows,) * 7 + (P(None, "tensor"),) * 3 + (P("tensor"),) * 4 + (P(), P()),
        out_specs=(P("seq", "tensor"), P("seq", "tensor"), P("tensor"), P("tensor")),
        check_vma=False,
    )
```

time: 187 us -> 62.8 us (0.34)
  Pallas kernels: 0 us -> 57.1 us
  blocking collectives: 55.4 us -> 0 us
  starting transfers between devices: 36.3 us -> 0 us
  other arithmetic: 30.3 us -> 0 us
  between operations: 19 us -> 0.66 us
  waiting for transfers between devices: 14.2 us -> 0 us
  local copies, waits for them, and re-layouts: 16.8 us -> 3.83 us
  matrix products: 12.8 us -> 0 us
    pallas_call x0 -> x1, Pallas kernels: none -> 57.1 us  [local(): pl.pallas_call(functools.partial(kernel, S, T), out_shape=(jax.ShapeDtype...]
    all_gather x3 -> x0, blocking collectives: 31.8 us -> none  [the longest x1 12.8 us: prefix(): lax.all_gather(part.astype(kind), axis)]
    all_to_all x7 -> x0, starting transfers between devices: 31.4 us -> none  [the longest x1 6.35 us: local(): lax.all_to_all(mamba_dt, 'tensor', split_axis=1, concat_axis=0, tiled=True)]
    psum x1 -> x0, blocking collectives: 23.6 us -> none  [local(): lax.psum((jnp.sum(attention.astype(jnp.float32), axis=0), jnp.sum(mamba_o...]
    all_to_all x7 -> x0, waiting for transfers between devices: 13.8 us -> none  [the longest x1 8.17 us: local(): lax.all_to_all(mamba_x, 'tensor', split_axis=1, concat_axis=0, tiled=True)]
    dot_general x6 -> x0, matrix products: 12.8 us -> none  [the longest x1 4.35 us: compute(): jnp.einsum('gqts,sgd->gqtd', weights.astype(jnp.bfloat16), values_rank3,...]
    select_n x8 -> x0, other arithmetic: 10.4 us -> none  [turn(): return jax.tree.map(lambda a, b: jnp.where(reached, a, b), new, before)]
    convert_element_type x12 -> x0, other arithmetic: 8.45 us -> none  [the longest x8 5.54 us: turn(): part[k].astype(own.dtype)]
  transfers between devices with their start and end apart: 11 -> 0, of which waited for: 4 -> 0; matrix products, arithmetic and copies ran while one was open for 20% -> 0% of each run, Pallas kernels for 0% -> 0%
where the time goes in v1:
time: 62.8 us; the launch traced here: 61.6 us
  Pallas kernels  57.1 us (91%)
  local copies, waits for them, and re-layouts  3.83 us (6%)
  between operations  0.66 us (1%)
    pallas_call x1, Pallas kernels, local(): pl.pallas_call(functools.partial(kernel, S, T), out_shape=(jax.ShapeDtype...  57.1 us
    unnamed x10, local copies, waits for them, and re-layouts  3.83 us

profile of v1, /device:TPU:0, one launch (start us, length us, event | category | flops | bytes accessed | tf_op | source)
XLA Modules:
  0.0 61.6 jit_solution(11797262561850232730)
XLA Ops:
  0.6 57.1 %shard_map.183 = (bf16[128,1024]{1,0:T(8,128)(2,1)}, bf16[128,2048]{1,0:T(8,128)(2,1)}, f32[1,1024]{1,0:T(1,128)}, f32[1,2048]{1,0:T(1,128)}) custom-call(bf16[32,4096]{1,0:T(8,128)(2,1)} %q_in.1, bf16[32,1024]{1,0:T(8,128)(2,1)} %k_in.1, bf16[32,1024]{1,0:T(8,128)(2,1)} %v_in.1, bf16[32,8192]{1,0:T(8,128)(2,1)} %x_in.1, bf16[32,1024]{1,0:T(8,128)(2,1)} %b_in.1, ...), custom_call_target="tpu_custom_call" | custom-call | tf_op jit(solution)/shard_map/pallas_call | solution.py:613
  57.8 0.0 copy-start
  57.8 1.7 %copy.24 = bf16[128,1024]{1,0:T(8,128)(2,1)} copy(bf16[128,1024]{1,0:T(8,128)(2,1)} %get-tuple-element.16) | data formatting | bytes 524288
  59.5 0.0 copy-done
  59.5 0.0 copy-start.2
  59.5 0.8 %copy.25 = bf16[128,2048]{1,0:T(8,128)(2,1)} copy(bf16[128,2048]{1,0:T(8,128)(2,1)S(1)} %copy-done) | data formatting | bytes 1048576
  60.3 0.0 copy-done.2
  60.3 0.0 copy-start.1
  60.3 0.6 copy.26
  60.9 0.1 copy-done.1
  61.0 0.6 copy.27
Async XLA Ops:
  57.8 1.7 %copy-start = (bf16[128,2048]{1,0:T(8,128)(2,1)S(1)}, bf16[128,2048]{1,0:T(8,128)(2,1)}, u32[]{:S(2)}) copy-start(bf16[128,2048]{1,0:T(8,128)(2,1)} %get-tuple-element.17) | copy-start | bytes 1572868
  59.5 0.8 %copy-start.2 = (f32[1,1024]{1,0:T(1,128)S(1)}, f32[1,1024]{1,0:T(1,128)}, u32[]{:S(2)}) copy-start(f32[1,1024]{1,0:T(1,128)} %get-tuple-element.10) | copy-start | bytes 12292
  60.3 0.7 %copy-start.1 = (f32[1,2048]{1,0:T(1,128)S(1)}, f32[1,2048]{1,0:T(1,128)}, u32[]{:S(2)}) copy-start(f32[1,2048]{1,0:T(1,128)} %get-tuple-element.11) | copy-start | bytes 24580

commit v2 on v1

--- a/solution.py
+++ b/solution.py
@@ -101,7 +101,6 @@
     gfac,
     fexp,
     ret,
-    incf,
     incoming,
     sums,
     a_send,
@@ -150,6 +149,9 @@
     pl.semaphore_wait(barrier, T - 1 + S - 1)
 
     base = me * rows
+    NP = st_send.shape[0]
+    pw = xw // NP
+    Q = 5 + NP
 
     def dst_of(a, source):
         if a == 0:
@@ -163,17 +165,19 @@
             return xbc.at[ext, pl.ds(xw, bw)]
         if a == 4:
             return xbc.at[ext, pl.ds(xw + bw, bw)]
-        if a == 5:
-            return xbc.at[ext, pl.ds(0, xw)]
+        if a < 5 + NP:
+            return xbc.at[ext, pl.ds((a - 5) * pw, pw)]
         return qbuf.at[pl.ds(pl.multiple_of(source * piece, piece), piece), :]
 
-    ins = (k_in, v_in, dt_in, b_in, c_in, x_in, q_in)
-    widths = (kw, kw, None, bw, bw, xw, qw)
+    ins = (k_in, v_in, dt_in, b_in, c_in) + (x_in,) * NP + (q_in,)
+    widths = (kw, kw, None, bw, bw) + (xw,) * NP + (qw,)
 
     def src_of(a, target):
         if widths[a] is None:
             return ins[a].at[:, :]
         w = widths[a]
+        if 5 <= a < Q:
+            return x_in.at[:, pl.ds(pl.multiple_of(target * w + (a - 5) * pw, pw), pw)]
         return ins[a].at[:, pl.ds(pl.multiple_of(target * w, w), w)]
 
     def a2a_send(a, d):
@@ -191,8 +195,14 @@
                 src_of(a, mt), dst_of(a, source), a_send.at[a, d], a_recv.at[a, d], "tensor", source
             ).wait_recv()
 
-    for a in range(7):
-        for d in range(1, T):
+    low = mt < (T + 1) // 2
+    order = []
+    for e in range(T - 1):
+        down = jnp.where(T - 1 - e > mt, T - 1 - e, T - 2 - e)
+        up = jnp.where(e < mt, e, e + 1)
+        order.append(lax.rem(jnp.where(low, down, up) - mt + T, T))
+    for a in (2, 3, 4, 0, 1, *range(5, Q + 1)):
+        for d in order:
             a2a_send(a, d).start()
         a2a_local(a).start()
 
@@ -219,21 +229,6 @@
         return carry
 
     lax.fori_loop(0, n_chunks, gap_chunk, 0)
-
-    a2a_wait(0)
-    a2a_wait(1)
-
-    def kv_block(owner):
-        return kv.at[pl.ds(pl.multiple_of(owner * rows, rows), rows), :]
-
-    def kv_copy(d, owner, peer):
-        return rdma(kv_block(owner), kv_block(owner), kv_send.at[d], kv_recv.at[d], "seq", peer)
-
-    def kv_start(d, carry):
-        kv_copy(d, me, lax.rem(me + d, S)).start()
-        return carry
-
-    lax.fori_loop(1, S, kv_start, 0)
 
     a2a_wait(2)
     hot = (iota((LANES, heads), 0) == iota((LANES, heads), 1) + mt * heads).astype(BF16)
@@ -257,31 +252,85 @@
     factor = jnp.where(prior_doc == last_doc, jnp.exp(ending), 0.0)
     fac[...] = jnp.broadcast_to(factor, fac.shape)
     inflow = jnp.where(docs == prior_doc, jnp.exp(cum), 0.0)
-    te = parts3(to_end)
-    inf = parts3(inflow)
+    te = parts3(to_end)[:2]
+    inf = parts3(inflow)[:2]
+
+    def f_copy(d, owner, peer):
+        return rdma(fac, gfac.at[owner], f_send.at[d], f_recv.at[d], "seq", peer)
+
+    is_holder = lax.rem(me, stride) == 0
+
+    def f_start(d, carry):
+        peer = lax.rem(me + d, S)
+
+        @pl.when(lax.rem(peer, stride) == 0)
+        def _():
+            f_copy(d, me, peer).start()
+
+        return carry
+
+    lax.fori_loop(1, S, f_start, 0)
+    gfac[me] = fac[...]
 
     a2a_wait(3)
     a2a_wait(4)
-    a2a_wait(5)
-
-    def tail_copy(peer):
+
+    def tail_copy(p, peer):
+        lanes = pl.ds(p * pw, pw) if p < NP else pl.ds(xw, 2 * bw)
         return rdma(
-            xbc.at[pl.ds(rows, TAIL), :], xbc.at[pl.ds(0, TAIL), :],
-            tail_sem.at[0], tail_sem.at[1], "seq", peer,
-        )
-
-    @pl.when(me < S - 1)
-    def _():
-        tail_copy(lax.rem(me + 1, S)).start()
-
-    @pl.when(me > 0)
-    def _():
-        tail_copy(lax.rem(me + S - 1, S)).wait_recv()
+            xbc.at[pl.ds(rows, TAIL), lanes], xbc.at[pl.ds(0, TAIL), lanes],
+            tail_sem.at[p, 0], tail_sem.at[p, 1], "seq", peer,
+        )
+
+    def tail_start(p):
+        @pl.when(me < S - 1)
+        def _():
+            tail_copy(p, lax.rem(me + 1, S)).start()
+
+    def tail_wait(p):
+        @pl.when(me > 0)
+        def _():
+            tail_copy(p, lax.rem(me + S - 1, S)).wait_recv()
 
     @pl.when(me == 0)
     def _():
         xbc[pl.ds(0, TAIL), :] = jnp.zeros((TAIL, xbc.shape[1]), BF16)
 
+    tail_start(NP)
+
+    a2a_wait(0)
+    a2a_wait(1)
+
+    twin = me + 1 - 2 * lax.rem(me, 2)
+
+    def kv_block(owner):
+        return kv.at[pl.ds(pl.multiple_of(owner * rows, rows), rows), :]
+
+    def kv_copy(d, owner, peer):
+        return rdma(kv_block(owner), kv_block(owner), kv_send.at[d], kv_recv.at[d], "seq", peer)
+
+    def kv_start(e, carry):
+        kv_copy(e, me, lax.rem(me + 2 * e, S)).start()
+        return carry
+
+    lax.fori_loop(1, S // 2, kv_start, 0)
+    kv_copy(0, me, twin).start()
+
+    @pl.when(is_holder)
+    def _():
+        def arrive(d, carry):
+            owner = lax.rem(me + S - d, S)
+            f_copy(d, owner, owner).wait_recv()
+            return carry
+
+        lax.fori_loop(1, S, arrive, 0)
+        spread = (iota((heads, xw), 0) == iota((heads, xw), 1) // MP).astype(BF16)
+        fp = parts3(gfac[...].reshape(S * 8, heads))
+        fexp[...] = (mm(fp[0], spread) + mm(fp[1], spread) + mm(fp[2], spread)).reshape(
+            S, 8, xw
+        )
+
+    tail_wait(NP)
     width = 256 if xw % 256 == 0 and bw % 256 == 0 else 128
     pos = base + iota((rows, 1), 0)
     keeps = []
@@ -309,59 +358,50 @@
         cg = bcbuf[:, bw + g * MN : bw + (g + 1) * MN]
         crossm[g] = jnp.where(causal, mm_t(cg, bg), 0.0)
 
-    for g in range(groups):
-        bt = bcbuf[:, g * MN : (g + 1) * MN].astype(F32).T.astype(BF16)
-        gw = per_group * MP
-
-        def stretch(i, carry, g=g, gw=gw, bt=bt):
-            lane = pl.multiple_of(g * gw + i * width, width)
-            out = conv(lane, conv_x, lane)
-            xc[:, pl.ds(lane, width)] = out
-            spread = (
-                iota((heads, width), 0) == (lane + iota((heads, width), 1)) // MP
-            ).astype(BF16)
-            to_end_x = mm(te[0], spread) + mm(te[1], spread) + mm(te[2], spread)
-            inflow_ref[:, pl.ds(lane, width)] = (
-                mm(inf[0], spread) + mm(inf[1], spread) + mm(inf[2], spread)
-            )
-            weighted = (to_end_x * out.astype(F32)).astype(BF16)
-            state[:, pl.ds(lane, width)] = mm(bt, weighted).astype(BF16)
+    bts = [
+        bcbuf[:, g * MN : (g + 1) * MN].astype(F32).T.astype(BF16) for g in range(groups)
+    ]
+    gw = per_group * MP
+
+    def stretch(lane):
+        out = conv(lane, conv_x, lane)
+        xc[:, lane : lane + width] = out
+        spread = (
+            iota((heads, width), 0) == (lane + iota((heads, width), 1)) // MP
+        ).astype(BF16)
+        inflow_ref[:, lane : lane + width] = mm(inf[0], spread) + mm(inf[1], spread)
+        weighted = ((mm(te[0], spread) + mm(te[1], spread)) * out.astype(F32)).astype(BF16)
+        state[:, lane : lane + width] = mm(bts[lane // gw], weighted).astype(BF16)
+
+    def st_copy(p, d, holder, owner, peer):
+        lanes = pl.ds(p * pw, pw)
+        return rdma(
+            state.at[pl.ds(pl.multiple_of(holder * srows, srows), srows), lanes],
+            gstate.at[owner, :, lanes], st_send.at[p, d], st_recv.at[p, d], "seq", peer,
+        )
+
+    def st_local(p):
+        lanes = pl.ds(p * pw, pw)
+        return pltpu.make_async_copy(
+            state.at[pl.ds(pl.multiple_of((me // stride) * srows, srows), srows), lanes],
+            gstate.at[me, :, lanes], st_recv.at[p, 0],
+        )
+
+    def st_issue(p):
+        def st_start(d, carry):
+            peer = lax.rem(me + d, S)
+
+            @pl.when(lax.rem(peer, stride) == 0)
+            def _():
+                st_copy(p, d, peer // stride, me, peer).start()
+
             return carry
 
-        lax.fori_loop(0, gw // width, stretch, 0)
-
-    def st_copy(d, holder, owner, peer):
-        return rdma(
-            state.at[pl.ds(pl.multiple_of(holder * srows, srows), srows), :],
-            gstate.at[owner], st_send.at[d], st_recv.at[d], "seq", peer,
-        )
-
-    def f_copy(d, owner, peer):
-        return rdma(fac, gfac.at[owner], f_send.at[d], f_recv.at[d], "seq", peer)
-
-    def st_local():
-        return pltpu.make_async_copy(
-            state.at[pl.ds(pl.multiple_of((me // stride) * srows, srows), srows), :],
-            gstate.at[me], st_recv.at[0],
-        )
-
-    def st_start(d, carry):
-        peer = lax.rem(me + d, S)
-
-        @pl.when(lax.rem(peer, stride) == 0)
+        lax.fori_loop(1, S, st_start, 0)
+
+        @pl.when(is_holder)
         def _():
-            st_copy(d, peer // stride, me, peer).start()
-            f_copy(d, me, peer).start()
-
-        return carry
-
-    lax.fori_loop(1, S, st_start, 0)
-    is_holder = lax.rem(me, stride) == 0
-
-    @pl.when(is_holder)
-    def _():
-        st_local().start()
-        gfac[me] = fac[...]
+            st_local(p).start()
 
     half = iota((1, 2 * MP), 1) < MP
 
@@ -386,64 +426,85 @@
         )
         return carry
 
-    lax.fori_loop(0, heads // 2, intra, 0)
-
-    def ret_copy(d, target, holder, peer):
+    pairs = heads // 2 // NP
+
+    def intra_piece(p):
+        lax.fori_loop(p * pairs, (p + 1) * pairs, intra, 0, unroll=2)
+
+    for p in range(NP):
+        a2a_wait(5 + p)
+        tail_start(p)
+        if p > 0:
+            intra_piece(p - 1)
+        tail_wait(p)
+        for i in range(pw // width):
+            stretch(p * pw + i * width)
+        st_issue(p)
+    intra_piece(NP - 1)
+
+    def kv_pass(e, carry):
+        owner = lax.rem(me + S - 2 * e, S)
+        kv_copy(e, owner, owner).wait_recv()
+        kv_copy(S // 2 + e, owner, twin).start()
+        return carry
+
+    lax.fori_loop(1, S // 2, kv_pass, 0)
+
+    def ret_copy(p, d, target, holder, peer):
+        lanes = pl.ds(p * pw, pw)
         return rdma(
-            ret.at[target],
-            incoming.at[pl.ds(pl.multiple_of(holder * srows, srows), srows), :],
-            r_send.at[d], r_recv.at[d], "seq", peer,
-        )
-
-    def ret_local():
+            ret.at[target, :, lanes],
+            incoming.at[pl.ds(pl.multiple_of(holder * srows, srows), srows), lanes],
+            r_send.at[p, d], r_recv.at[p, d], "seq", peer,
+        )
+
+    def ret_local(p):
+        lanes = pl.ds(p * pw, pw)
         return pltpu.make_async_copy(
-            ret.at[me],
-            incoming.at[pl.ds(pl.multiple_of((me // stride) * srows, srows), srows), :],
-            r_recv.at[0],
-        )
-
-    @pl.when(is_holder)
-    def _():
-        st_local().wait()
-
-        def arrive(d, carry):
-            owner = lax.rem(me + S - d, S)
-            st_copy(d, me // stride, owner, owner).wait_recv()
-            f_copy(d, owner, owner).wait_recv()
-            return carry
-
-        lax.fori_loop(1, S, arrive, 0)
-        spread = (iota((heads, xw), 0) == iota((heads, xw), 1) // MP).astype(BF16)
-        fp = parts3(gfac[...].reshape(S * 8, heads))
-        fexp[...] = (mm(fp[0], spread) + mm(fp[1], spread) + mm(fp[2], spread)).reshape(
-            S, 8, xw
-        )
-        incf[...] = jnp.zeros_like(incf)
-
-        def scan(k, carry):
-            now = incf[...]
-            ret[k] = now.astype(BF16)
-            incf[...] = fexp[k][0:1, :] * now + gstate[k].astype(F32)
-            return carry
-
-        lax.fori_loop(0, S, scan, 0)
-        ret_local().start()
-
-        def give(d, carry):
-            peer = lax.rem(me + d, S)
-            ret_copy(d, peer, me // stride, peer).start()
-            return carry
-
-        lax.fori_loop(1, S, give, 0)
-
-    a2a_wait(6)
-
-    def kv_wait(d, carry):
-        owner = lax.rem(me + S - d, S)
-        kv_copy(d, owner, owner).wait_recv()
-        return carry
-
-    lax.fori_loop(1, S, kv_wait, 0)
+            ret.at[me, :, lanes],
+            incoming.at[pl.ds(pl.multiple_of((me // stride) * srows, srows), srows), lanes],
+            r_recv.at[p, 0],
+        )
+
+    def prefix_piece(p):
+        lanes = slice(p * pw, (p + 1) * pw)
+
+        @pl.when(is_holder)
+        def _():
+            st_local(p).wait()
+
+            def arrive(d, carry):
+                owner = lax.rem(me + S - d, S)
+                st_copy(p, d, me // stride, owner, owner).wait_recv()
+                return carry
+
+            lax.fori_loop(1, S, arrive, 0)
+
+            def scan(k, now):
+                ret[k, :, lanes] = now.astype(BF16)
+                return fexp[k, 0:1, lanes] * now + gstate[k, :, lanes].astype(F32)
+
+            lax.fori_loop(0, S, scan, jnp.zeros((srows, pw), F32))
+            ret_local(p).start()
+
+            def give(d, carry):
+                peer = lax.rem(me + d, S)
+                ret_copy(p, d, peer, me // stride, peer).start()
+                return carry
+
+            lax.fori_loop(1, S, give, 0)
+
+    for p in range(NP):
+        prefix_piece(p)
+
+    a2a_wait(Q)
+
+    def kv_wait(e, carry):
+        kv_copy(S // 2 + e, lax.rem(twin + S - 2 * e, S), twin).wait_recv()
+        return carry
+
+    lax.fori_loop(1, S // 2, kv_wait, 0)
+    kv_copy(0, twin, twin).wait_recv()
 
     to_exp2 = math.log2(math.e) / math.sqrt(HEAD_SIZE)
     width_of_group = qheads // (kw // HEAD_SIZE)
@@ -497,20 +558,21 @@
 
     lax.fori_loop(0, qheads // 2, attend, 0)
 
-    def collect(h, carry):
-        @pl.when(h * stride != me)
+    def collect_piece(p):
+        def collect(h, carry):
+            @pl.when(h * stride != me)
+            def _():
+                peer = h * stride
+                d = lax.rem(me - peer + S, S)
+                ret_copy(p, d, me, h, peer).wait_recv()
+
+            return carry
+
+        lax.fori_loop(0, holders, collect, 0)
+
+        @pl.when(is_holder)
         def _():
-            peer = h * stride
-            d = lax.rem(me - peer + S, S)
-            ret_copy(d, me, h, peer).wait_recv()
-
-        return carry
-
-    lax.fori_loop(0, holders, collect, 0)
-
-    @pl.when(is_holder)
-    def _():
-        ret_local().wait()
+            ret_local(p).wait()
 
     pair = 2 * MP
     ones = (iota((pair, pair), 0) // MP == iota((pair, pair), 1) // MP).astype(BF16)
@@ -522,7 +584,7 @@
         entering = mm(cg, incoming[:, pl.ds(lane, pair)])
         y = full[:, pl.ds(lane, pair)] + entering * inflow_ref[:, pl.ds(lane, pair)]
         p = parts3(y * y)
-        mean = (mm(p[0], ones) + mm(p[1], ones) + mm(p[2], ones)) * (1.0 / MP)
+        mean = (mm(p[0], ones) + mm(p[1], ones)) * (1.0 / MP)
         o = (y * lax.rsqrt(mean + EPS_NORM) * gain_ref[:, pl.ds(lane, pair)]).astype(BF16)
         mamba_ref[:, pl.ds(lane, pair)] = o
         sums[me, :, pl.ds(pl.multiple_of(qw + lane, pair), pair)] = jnp.sum(
@@ -530,7 +592,9 @@
         )
         return carry
 
-    lax.fori_loop(0, heads // 2, finish, 0)
+    for p in range(NP):
+        collect_piece(p)
+        lax.fori_loop(p * pairs, (p + 1) * pairs, finish, 0, unroll=2)
 
     def sum_copy(d, owner, peer):
         return rdma(sums.at[owner], sums.at[owner], c_send.at[d], c_recv.at[d], "seq", peer)
@@ -541,30 +605,40 @@
 
     lax.fori_loop(1, S, sum_start, 0)
 
-    for a in range(7):
+    for a in range(Q + 1):
         for d in range(1, T):
             a2a_send(a, d).wait_send()
 
     @pl.when(me < S - 1)
     def _():
-        tail_copy(lax.rem(me + 1, S)).wait_send()
+        for p in range(NP + 1):
+            tail_copy(p, lax.rem(me + 1, S)).wait_send()
 
     def drain(d, carry):
         peer = lax.rem(me + d, S)
-        kv_copy(d, me, peer).wait_send()
 
         @pl.when(lax.rem(peer, stride) == 0)
         def _():
-            st_copy(d, peer // stride, me, peer).wait_send()
+            for p in range(NP):
+                st_copy(p, d, peer // stride, me, peer).wait_send()
             f_copy(d, me, peer).wait_send()
 
         @pl.when(is_holder)
         def _():
-            ret_copy(d, peer, me // stride, peer).wait_send()
+            for p in range(NP):
+                ret_copy(p, d, peer, me // stride, peer).wait_send()
 
         return carry
 
     lax.fori_loop(1, S, drain, 0)
+
+    def kv_drain(e, carry):
+        kv_copy(e, me, lax.rem(me + 2 * e, S)).wait_send()
+        kv_copy(S // 2 + e, lax.rem(me + S - 2 * e, S), twin).wait_send()
+        return carry
+
+    lax.fori_loop(1, S // 2, kv_drain, 0)
+    kv_copy(0, me, twin).wait_send()
 
     def sum_wait(d, carry):
         owner = lax.rem(me + S - d, S)
@@ -607,16 +681,17 @@
     heads = xw // MP
     holders = min(S, MN // 16)
     srows = MN // holders
+    pieces = xw // 512 if xw % 512 == 0 else 1
     vmem = pl.BlockSpec(memory_space=pltpu.VMEM)
     smem = pl.BlockSpec(memory_space=pltpu.SMEM)
     dma = pltpu.SemaphoreType.DMA
     attn, mamba, asum, msum = pl.pallas_call(
         functools.partial(kernel, S, T),
         out_shape=(
-            jax.ShapeDtypeStruct((rows, qw), BF16),
-            jax.ShapeDtypeStruct((rows, xw), BF16),
-            jax.ShapeDtypeStruct((1, qw), F32),
-            jax.ShapeDtypeStruct((1, xw), F32),
+            pltpu.VMEM((rows, qw), BF16),
+            pltpu.VMEM((rows, xw), BF16),
+            pltpu.VMEM((1, qw), F32),
+            pltpu.VMEM((1, xw), F32),
         ),
         in_specs=[vmem] * 13 + [smem] * 3,
         out_specs=(vmem,) * 4,
@@ -640,20 +715,19 @@
             pltpu.VMEM((S, 8, heads), F32),
             pltpu.VMEM((S, 8, xw), F32),
             pltpu.VMEM((S, srows, xw), BF16),
-            pltpu.VMEM((srows, xw), F32),
             pltpu.VMEM((MN, xw), BF16),
             pltpu.VMEM((S, 1, qw + xw), F32),
-            dma((7, T)),
-            dma((7, T)),
+            dma((6 + pieces, T)),
+            dma((6 + pieces, T)),
             dma((S,)),
             dma((S,)),
-            dma((2,)),
+            dma((pieces + 1, 2)),
+            dma((pieces, S)),
+            dma((pieces, S)),
             dma((S,)),
             dma((S,)),
-            dma((S,)),
-            dma((S,)),
-            dma((S,)),
-            dma((S,)),
+            dma((pieces, S)),
+            dma((pieces, S)),
             dma((S,)),
             dma((S,)),
         ],

time: 62.8 us -> 52.5 us (0.84); the launches traced: 61.6 us -> 52.4 us
  Pallas kernels: 57.1 us -> 49.1 us
  local copies, waits for them, and re-layouts: 3.83 us -> 2.69 us
    pallas_call x1, Pallas kernels: 57.1 us -> 49.1 us  [local(): pl.pallas_call(functools.partial(kernel, S, T), out_shape=(pltpu.VMEM((ro...]
    unnamed x10 -> x4, local copies, waits for them, and re-layouts: 3.83 us -> 2.69 us
where the time goes in v2:
time: 52.5 us; the launch traced here: 52.4 us
  Pallas kernels  49.1 us (94%)
  local copies, waits for them, and re-layouts  2.69 us (5%)
  between operations  0.65 us (1%)
    pallas_call x1, Pallas kernels, local(): pl.pallas_call(functools.partial(kernel, S, T), out_shape=(pltpu.VMEM((ro...  49.1 us
    unnamed x4, local copies, waits for them, and re-layouts  2.69 us

profile of v2, /device:TPU:0, one launch (start us, length us, event | category | flops | bytes accessed | tf_op | source)
XLA Modules:
  0.0 52.4 jit_solution(16418813695609612840)
XLA Ops:
  0.6 49.1 %shard_map.183 = (bf16[128,1024]{1,0:T(8,128)(2,1)S(1)}, bf16[128,2048]{1,0:T(8,128)(2,1)S(1)}, f32[1,1024]{1,0:T(1,128)S(1)}, f32[1,2048]{1,0:T(1,128)S(1)}) custom-call(bf16[32,4096]{1,0:T(8,128)(2,1)} %q_in.1, bf16[32,1024]{1,0:T(8,128)(2,1)} %k_in.1, bf16[32,1024]{1,0:T(8,128)(2,1)} %v_in.1, bf16[32,8192]{1,0:T(8,128)(2,1)} %x_in.1, ...), custom_call_target="tpu_custom_call" | custom-call | tf_op jit(solution)/shard_map/pallas_call | solution.py:688
  49.7 0.7 %copy.24 = bf16[128,1024]{1,0:T(8,128)(2,1)} copy(bf16[128,1024]{1,0:T(8,128)(2,1)S(1)} %get-tuple-element.12) | data formatting | bytes 524288
  50.4 0.6 %copy.26 = f32[1024]{0:T(1024)} copy(f32[1024]{0:T(1024)S(1)} %bitcast.6) | data formatting | bytes 8192
  51.0 0.6 %copy.27 = f32[2048]{0:T(1024)} copy(f32[2048]{0:T(1024)S(1)} %bitcast.5) | data formatting | bytes 16384
  51.6 0.8 %copy.25 = bf16[128,2048]{1,0:T(8,128)(2,1)} copy(bf16[128,2048]{1,0:T(8,128)(2,1)S(1)} %get-tuple-element.13) | data formatting | bytes 1048576
